TPU v7x, 32 devices: a whole 2x2x4 slice. The times are simulated.
32 devices in a mesh: pix: 8 (over z, x), frm: 4 (over y, core).
Axes of the slice: x: 2, y: 2, z: 4, core: 2. Of those that a mesh axis runs over, the one named last changes fastest.
Arguments:
- frames_y: bfloat16 [1024, 2048], P('pix', 'frm'), may hold values from -6 to 6
- traces: bfloat16 [1024, 2048], P('pix', 'frm'), may hold values from -0.13183594 to 0.13183594
- footprints: float32 [1024, 1024], P('pix'), may hold values from 0 to 2
- order: int32 [1024], replicated, may hold values from 0 to 1023, each once
- support: int32 [8, 256], P('pix'), may hold values from 0 to 1023, as said below
Outputs:
- footprints_new: float32 [1024, 1024], P('pix')
Inputs may be any that keep to these rules, and one draw needn't show every extreme that they name: `support`: row j lists 256 different neurons; it governs pixels j * 128 to (j + 1) * 128 - 1.
All inputs are finite; a program needn't handle non-finite values.
Results may differ from a plain program's by a relative error of at most 0.0003.
Values may be sent and summed in bfloat16 or wider, within the bound.
No kernel may reach another device: no remote copies, remote signals or barrier semaphores. Data moves between devices by JAX's collectives and lax.ppermute only.
A program may use at most 64 MiB of HBM per device.

v0:
```python
import jax
import jax.numpy as jnp
from jax import lax
from jax.sharding import PartitionSpec as P

BLK = 128
SWEEPS = 3


def local(frames_y, traces, footprints, order, support):
    highest = lax.Precision.HIGHEST
    pix_rows = frames_y.shape[0]
    neurons = footprints.shape[1]
    total_pixels = pix_rows * lax.axis_size("pix")
    contract = (((1,), (1,)), ((), ()))
    stacked = jnp.concatenate([frames_y, traces], axis=0)
    terms = lax.dot_general(
        stacked,
        lax.all_gather(traces, "pix", axis=0, tiled=True),
        contract,
        preferred_element_type=jnp.float32,
    )
    cross, gram_part = lax.psum((terms[:pix_rows], terms[pix_rows:]), "frm")
    gram = lax.all_gather(gram_part, "pix", axis=0, tiled=True)
    neuron_ids = lax.iota(jnp.int32, neurons)
    member = jnp.any(support[0][:, None] == neuron_ids[None, :], axis=0).astype(jnp.float32)
    keep_perm = jnp.take(member, order)
    current = jnp.take(footprints, order, axis=1)
    cross_perm = jnp.take(cross, order, axis=1)
    gram_perm = jnp.take(jnp.take(gram, order, axis=0), order, axis=1)
    diagonal = jnp.diagonal(gram_perm)
    block_count = neurons // BLK
    for sweep_index in range(SWEEPS):
        for block_index in range(block_count):
            lower = block_index * BLK
            upper = lower + BLK
            numer = cross_perm[:, lower:upper] - jnp.dot(
                current, gram_perm[:, lower:upper], precision=highest
            )
            update = keep_perm[lower:upper] * jnp.maximum(
                current[:, lower:upper] + numer / diagonal[lower:upper], 0.0
            )
            squares = lax.psum(jnp.sum(update * update, axis=0), "pix")
            scale = jnp.sqrt(squares / total_pixels + 1e-06)
            current = current.at[:, lower:upper].set(update / scale)
    return jnp.zeros_like(current).at[:, order].set(current)


def solution(mesh):
    in_specs = (P("pix", "frm"), P("pix", "frm"), P("pix", None), P(), P("pix", None))
    out_specs = P("pix", None)
    return jax.shard_map(local, mesh=mesh, in_specs=in_specs, out_specs=out_specs, check_vma=False)
```

profile of v0, /device:TPU:0, one launch (start us, length us, event | category | flops | bytes accessed | tf_op | source)
XLA Modules:
  0.0 714.0 jit_solution(11070790319049338248)
XLA Ops:
  7.3 45.2 %all-gather.3.cloned.1.call-done = bf16[1024,512]{1,0:T(8,128)(2,1)} async-done(((bf16[128,512]{1,0:T(8,128)(2,1)}), bf16[1024,512]{1,0:T(8,128)(2,1)}) %all-gather.3.cloned.1.call-update) | async-done | bytes 1048592 | tf_op jit(solution)/shard_map/all_gather | solution.py:19
  55.4 35.2 %all-reduce.3.cloned.1.call-done = (f32[128,1024]{1,0:T(8,128)}, f32[128,1024]{1,0:T(8,128)}) async-done(((f32[128,1024]{1,0:T(8,128)}, f32[128,1024]{1,0:T(8,128)}), (f32[128,1024]{1,0:T(8,128)}, f32[128,1024]{1,0:T(8,128)})) %all-reduce.3.cloned.1.call-update) | async-done | bytes 1048592 | tf_op jit(solution)/shard_map/psum | solution.py:23
  106.5 59.5 %all-gather.5.cloned.1.call-done = f32[1024,1024]{1,0:T(8,128)} async-done(((f32[128,1024]{1,0:T(8,128)}), f32[1024,1024]{1,0:T(8,128)}) %all-gather.5.cloned.1.call-update) | async-done | bytes 4194320 | tf_op jit(solution)/shard_map/all_gather | solution.py:24
  216.1 19.0 %psum.184 = f32[128]{0:T(128)S(1)} all-reduce(f32[128]{0:T(128)S(1)} %get-tuple-element.320), channel_id=1, replica_groups=mesh['pix'=8,'frm'=4] {'pix'}, use_global_device_ids=true, to_apply=%region_5.7 | all-reduce | flops 128 | bytes 1024 | tf_op jit(solution)/shard_map/psum | solution.py:43
  237.4 17.3 %psum.185 = f32[128]{0:T(128)S(1)} all-reduce(f32[128]{0:T(128)S(1)} %get-tuple-element.322), channel_id=1, replica_groups=mesh['pix'=8,'frm'=4] {'pix'}, use_global_device_ids=true, to_apply=%region_8.10 | all-reduce | flops 128 | bytes 1024 | tf_op jit(solution)/shard_map/psum | solution.py:43
  257.0 19.0 %psum.186 = f32[128]{0:T(128)S(1)} all-reduce(f32[128]{0:T(128)S(1)} %get-tuple-element.324), channel_id=1, replica_groups=mesh['pix'=8,'frm'=4] {'pix'}, use_global_device_ids=true, to_apply=%region_11.13 | all-reduce | flops 128 | bytes 1024 | tf_op jit(solution)/shard_map/psum | solution.py:43
  278.3 17.2 %psum.187 = f32[128]{0:T(128)S(1)} all-reduce(f32[128]{0:T(128)S(1)} %get-tuple-element.326), channel_id=1, replica_groups=mesh['pix'=8,'frm'=4] {'pix'}, use_global_device_ids=true, to_apply=%region_14.16 | all-reduce | flops 128 | bytes 1024 | tf_op jit(solution)/shard_map/psum | solution.py:43
  297.8 19.0 %psum.188 = f32[128]{0:T(128)S(1)} all-reduce(f32[128]{0:T(128)S(1)} %get-tuple-element.328), channel_id=1, replica_groups=mesh['pix'=8,'frm'=4] {'pix'}, use_global_device_ids=true, to_apply=%region_17.19 | all-reduce | flops 128 | bytes 1024 | tf_op jit(solution)/shard_map/psum | solution.py:43
  338.6 19.0 %psum.190 = f32[128]{0:T(128)S(1)} all-reduce(f32[128]{0:T(128)S(1)} %get-tuple-element.332), channel_id=1, replica_groups=mesh['pix'=8,'frm'=4] {'pix'}, use_global_device_ids=true, to_apply=%region_23.25 | all-reduce | flops 128 | bytes 1024 | tf_op jit(solution)/shard_map/psum | solution.py:43
  360.0 17.2 %psum.191 = f32[128]{0:T(128)S(1)} all-reduce(f32[128]{0:T(128)S(1)} %get-tuple-element.334), channel_id=1, replica_groups=mesh['pix'=8,'frm'=4] {'pix'}, use_global_device_ids=true, to_apply=%region_25.27 | all-reduce | flops 128 | bytes 1024 | tf_op jit(solution)/shard_map/psum | solution.py:43
  378.9 19.0 %psum.192 = f32[128]{0:T(128)S(1)} all-reduce(f32[128]{0:T(128)S(1)} %get-tuple-element.336), channel_id=1, replica_groups=mesh['pix'=8,'frm'=4] {'pix'}, use_global_device_ids=true, to_apply=%region_27.29 | all-reduce | flops 128 | bytes 1024 | tf_op jit(solution)/shard_map/psum | solution.py:43
  400.3 17.4 %psum.193 = f32[128]{0:T(128)S(1)} all-reduce(f32[128]{0:T(128)S(1)} %get-tuple-element.338), channel_id=1, replica_groups=mesh['pix'=8,'frm'=4] {'pix'}, use_global_device_ids=true, to_apply=%region_29.31 | all-reduce | flops 128 | bytes 1024 | tf_op jit(solution)/shard_map/psum | solution.py:43
  419.9 19.0 %psum.194 = f32[128]{0:T(128)S(1)} all-reduce(f32[128]{0:T(128)S(1)} %get-tuple-element.340), channel_id=1, replica_groups=mesh['pix'=8,'frm'=4] {'pix'}, use_global_device_ids=true, to_apply=%region_31.33 | all-reduce | flops 128 | bytes 1024 | tf_op jit(solution)/shard_map/psum | solution.py:43
  441.3 17.2 %psum.195 = f32[128]{0:T(128)S(1)} all-reduce(f32[128]{0:T(128)S(1)} %get-tuple-element.342), channel_id=1, replica_groups=mesh['pix'=8,'frm'=4] {'pix'}, use_global_device_ids=true, to_apply=%region_33.35 | all-reduce | flops 128 | bytes 1024 | tf_op jit(solution)/shard_map/psum | solution.py:43
  460.8 19.0 %psum.196 = f32[128]{0:T(128)S(1)} all-reduce(f32[128]{0:T(128)S(1)} %get-tuple-element.344), channel_id=1, replica_groups=mesh['pix'=8,'frm'=4] {'pix'}, use_global_device_ids=true, to_apply=%region_35.37 | all-reduce | flops 128 | bytes 1024 | tf_op jit(solution)/shard_map/psum | solution.py:43
  501.5 19.0 %psum.198 = f32[128]{0:T(128)S(1)} all-reduce(f32[128]{0:T(128)S(1)} %get-tuple-element.348), channel_id=1, replica_groups=mesh['pix'=8,'frm'=4] {'pix'}, use_global_device_ids=true, to_apply=%region_39.41 | all-reduce | flops 128 | bytes 1024 | tf_op jit(solution)/shard_map/psum | solution.py:43
  541.8 19.0 %psum.200 = f32[128]{0:T(128)S(1)} all-reduce(f32[128]{0:T(128)S(1)} %get-tuple-element.352), channel_id=1, replica_groups=mesh['pix'=8,'frm'=4] {'pix'}, use_global_device_ids=true, to_apply=%region_43.45 | all-reduce | flops 128 | bytes 1024 | tf_op jit(solution)/shard_map/psum | solution.py:43
  563.2 17.3 %psum.201 = f32[128]{0:T(128)S(1)} all-reduce(f32[128]{0:T(128)S(1)} %get-tuple-element.354), channel_id=1, replica_groups=mesh['pix'=8,'frm'=4] {'pix'}, use_global_device_ids=true, to_apply=%region_45.47 | all-reduce | flops 128 | bytes 1024 | tf_op jit(solution)/shard_map/psum | solution.py:43
  582.7 19.0 %psum.202 = f32[128]{0:T(128)S(1)} all-reduce(f32[128]{0:T(128)S(1)} %get-tuple-element.356), channel_id=1, replica_groups=mesh['pix'=8,'frm'=4] {'pix'}, use_global_device_ids=true, to_apply=%region_47.49 | all-reduce | flops 128 | bytes 1024 | tf_op jit(solution)/shard_map/psum | solution.py:43
  604.0 17.3 %psum.203 = f32[128]{0:T(128)S(1)} all-reduce(f32[128]{0:T(128)S(1)} %get-tuple-element.358), channel_id=1, replica_groups=mesh['pix'=8,'frm'=4] {'pix'}, use_global_device_ids=true, to_apply=%region_49.51 | all-reduce | flops 128 | bytes 1024 | tf_op jit(solution)/shard_map/psum | solution.py:43
  623.6 19.0 %psum.204 = f32[128]{0:T(128)S(1)} all-reduce(f32[128]{0:T(128)S(1)} %get-tuple-element.360), channel_id=1, replica_groups=mesh['pix'=8,'frm'=4] {'pix'}, use_global_device_ids=true, to_apply=%region_51.53 | all-reduce | flops 128 | bytes 1024 | tf_op jit(solution)/shard_map/psum | solution.py:43
  644.9 17.3 %psum.205 = f32[128]{0:T(128)S(1)} all-reduce(f32[128]{0:T(128)S(1)} %get-tuple-element.362), channel_id=1, replica_groups=mesh['pix'=8,'frm'=4] {'pix'}, use_global_device_ids=true, to_apply=%region_53.55 | all-reduce | flops 128 | bytes 1024 | tf_op jit(solution)/shard_map/psum | solution.py:43
  664.4 19.0 %psum.206 = f32[128]{0:T(128)S(1)} all-reduce(f32[128]{0:T(128)S(1)} %get-tuple-element.364), channel_id=1, replica_groups=mesh['pix'=8,'frm'=4] {'pix'}, use_global_device_ids=true, to_apply=%region_55.57 | all-reduce | flops 128 | bytes 1024 | tf_op jit(solution)/shard_map/psum | solution.py:43
  685.7 17.3 %psum.207 = f32[128]{0:T(128)S(1)} all-reduce(f32[128]{0:T(128)S(1)} %get-tuple-element.366), channel_id=1, replica_groups=mesh['pix'=8,'frm'=4] {'pix'}, use_global_device_ids=true, to_apply=%region_57.59 | all-reduce | flops 128 | bytes 1024 | tf_op jit(solution)/shard_map/psum | solution.py:43
  (121 shorter events, 176.9 us)
Async XLA Ops:
  6.5 84.1 %copy-start.3 = (s32[1,256]{1,0:T(1,128)S(1)}, s32[1,256]{1,0:T(1,128)}, u32[]{:S(2)}) copy-start(s32[1,256]{1,0:T(1,128)} %param.59) | copy-start | bytes 3076
  6.5 84.3 %copy-start = (f32[128,1024]{1,0:T(8,128)S(1)}, f32[128,1024]{1,0:T(8,128)}, u32[]{:S(2)}) copy-start(f32[128,1024]{1,0:T(8,128)} %param.57) | copy-start | bytes 1572868
  6.5 84.5 %copy-start.2 = (s32[1024]{0:T(1024)S(1)}, s32[1024]{0:T(1024)}, u32[]{:S(2)}) copy-start(s32[1024]{0:T(1024)} %param.58) | copy-start | bytes 12292
  6.5 46.0 %all-gather.3.cloned.1.call-start = ((), (), s32[]{:S(2)}) async-start(), calls=%async_computation | async-start | bytes 1179648 | tf_op jit(solution)/shard_map/all_gather | solution.py:19
  7.3 83.4 %all-reduce.3.cloned.1.call-start = ((), (), s32[]{:S(2)}) async-start(), calls=%async_computation.2 | async-start | bytes 2097152 | tf_op jit(solution)/shard_map/psum | solution.py:23
  55.4 110.7 %all-gather.5.cloned.1.call-start = ((), (), s32[]{:S(2)}) async-start(), calls=%async_computation.1 | async-start | bytes 4718592 | tf_op jit(solution)/shard_map/all_gather | solution.py:24
  91.1 12.1 %copy-start.1 = (f32[128,1024]{1,0:T(8,128)S(1)}, f32[128,1024]{1,0:T(8,128)}, u32[]{:S(2)}) copy-start(f32[128,1024]{1,0:T(8,128)} %get-tuple-element.295) | copy-start | bytes 1572868
Sparse Core Ops, SparseCore 0:
  9.5 42.9 all-gather.2
  55.5 35.0 all-reduce.2
  92.7 73.2 all-gather.4
where the time goes:
time: 717 us; the launch traced here: 714 us
  blocking collectives  435 us (61%)
  waiting for transfers between devices  141 us (20%)
  local copies, waits for them, and re-layouts  55.8 us (8%)
  matrix products  41.3 us (6%)
  other arithmetic  27.4 us (4%)
  between operations  13.5 us (2%)
    psum x24, blocking collectives, local(): squares = lax.psum(jnp.sum(update * update, axis=0), 'pix')  435 us
    all_gather x1, waiting for transfers between devices, local(): gram = lax.all_gather(gram_part, 'pix', axis=0, tiled=True)  59.5 us
    all_gather x1, waiting for transfers between devices, local(): lax.all_gather(traces, 'pix', axis=0, tiled=True)  45.2 us
    dot_general x24, matrix products, local(): jnp.dot(current, gram_perm[:, lower:upper], precision=highest)  39.5 us
    psum x1, waiting for transfers between devices, local(): cross, gram_part = lax.psum((terms[:pix_rows], terms[pix_rows:]), 'frm')  35.2 us
    gather x2, local copies, waits for them, and re-layouts, local(): gram_perm = jnp.take(jnp.take(gram, order, axis=0), order, axis=1)  17.2 us
    gather x1, local copies, waits for them, and re-layouts, local(): diagonal = jnp.diagonal(gram_perm)  16.8 us
  transfers between devices with their start and end apart: 3, of which 3 were waited for; matrix products, arithmetic and copies ran while one was open for 2% of the time, Pallas kernels for 0%

commit v1 on v0

--- a/solution.py
+++ b/solution.py
@@ -21,7 +21,12 @@
         preferred_element_type=jnp.float32,
     )
     cross, gram_part = lax.psum((terms[:pix_rows], terms[pix_rows:]), "frm")
-    gram = lax.all_gather(gram_part, "pix", axis=0, tiled=True)
+    ring = [gram_part]
+    for hop in range(7):
+        ring.append(lax.ppermute(ring[-1], "pix", [(dev, (dev + 1) % 8) for dev in range(8)]))
+    gram = jnp.roll(
+        jnp.concatenate(ring[::-1], axis=0), (lax.axis_index("pix") + 1) * ring[0].shape[0], axis=0
+    )
     neuron_ids = lax.iota(jnp.int32, neurons)
     member = jnp.any(support[0][:, None] == neuron_ids[None, :], axis=0).astype(jnp.float32)
     keep_perm = jnp.take(member, order)

time: 717 us -> 757 us (1.056)
  waiting for transfers between devices: 141 us -> 164 us
  local copies, waits for them, and re-layouts: 55.8 us -> 67.6 us
    ppermute x0 -> x7, waiting for transfers between devices: none -> 82.4 us  [local(): lax.ppermute(ring[-1], 'pix', [(dev, (dev + 1) % 8) for dev in range(8)])]
    all_gather x1 -> x0, waiting for transfers between devices: 59.5 us -> none  [local(): gram = lax.all_gather(gram_part, 'pix', axis=0, tiled=True)]
  transfers between devices with their start and end apart: 3 -> 9, of which waited for: 3 -> 8; matrix products, arithmetic and copies ran while one was open for 2% -> 3% of each run, Pallas kernels for 0% -> 0%
where the time goes in v1:
time: 757 us; the launch traced here: 754 us
  blocking collectives  438 us (58%)
  waiting for transfers between devices  164 us (22%)
  local copies, waits for them, and re-layouts  67.6 us (9%)
  matrix products  41.3 us (5%)
  other arithmetic  28.5 us (4%)
  between operations  13.9 us (2%)
    psum x24, blocking collectives, local(): squares = lax.psum(jnp.sum(update * update, axis=0), 'pix')  438 us
    ppermute x7, waiting for transfers between devices, local(): lax.ppermute(ring[-1], 'pix', [(dev, (dev + 1) % 8) for dev in range(8)])  82.4 us
    all_gather x1, waiting for transfers between devices, local(): lax.all_gather(traces, 'pix', axis=0, tiled=True)  45.2 us
    dot_general x24, matrix products, local(): jnp.dot(current, gram_perm[:, lower:upper], precision=highest)  39.5 us
    psum x1, waiting for transfers between devices, local(): cross, gram_part = lax.psum((terms[:pix_rows], terms[pix_rows:]), 'frm')  35.2 us
    gather x2, local copies, waits for them, and re-layouts, local(): gram_perm = jnp.take(jnp.take(gram, order, axis=0), order, axis=1)  17.2 us
    gather x1, local copies, waits for them, and re-layouts, local(): diagonal = jnp.diagonal(gram_perm)  16.8 us
  transfers between devices with their start and end apart: 9, of which 8 were waited for; matrix products, arithmetic and copies ran while one was open for 3% of the time, Pallas kernels for 0%

profile of v1, /device:TPU:0, one launch (start us, length us, event | category | flops | bytes accessed | tf_op | source)
XLA Modules:
  0.0 754.5 jit_solution(16506689867636812199)
XLA Ops:
  7.3 45.2 %all-gather.2.cloned.1.call-done = bf16[1024,512]{1,0:T(8,128)(2,1)} async-done(((bf16[128,512]{1,0:T(8,128)(2,1)}), bf16[1024,512]{1,0:T(8,128)(2,1)}) %all-gather.2.cloned.1.call-update) | async-done | bytes 1048592 | tf_op jit(solution)/shard_map/all_gather | solution.py:19
  55.4 35.2 %all-reduce.3.cloned.1.call-done = (f32[128,1024]{1,0:T(8,128)}, f32[128,1024]{1,0:T(8,128)}) async-done(((f32[128,1024]{1,0:T(8,128)}, f32[128,1024]{1,0:T(8,128)}), (f32[128,1024]{1,0:T(8,128)}, f32[128,1024]{1,0:T(8,128)})) %all-reduce.3.cloned.1.call-update) | async-done | bytes 1048592 | tf_op jit(solution)/shard_map/psum | solution.py:23
  253.7 21.8 %psum.184 = f32[128]{0:T(128)S(1)} all-reduce(f32[128]{0:T(128)S(1)} %get-tuple-element.320), channel_id=1, replica_groups=mesh['pix'=8,'frm'=4] {'pix'}, use_global_device_ids=true, to_apply=%region_5.7 | all-reduce | flops 128 | bytes 1024 | tf_op jit(solution)/shard_map/psum | solution.py:48
  277.8 17.1 %psum.185 = f32[128]{0:T(128)S(1)} all-reduce(f32[128]{0:T(128)S(1)} %get-tuple-element.322), channel_id=1, replica_groups=mesh['pix'=8,'frm'=4] {'pix'}, use_global_device_ids=true, to_apply=%region_8.10 | all-reduce | flops 128 | bytes 1024 | tf_op jit(solution)/shard_map/psum | solution.py:48
  297.2 19.1 %psum.186 = f32[128]{0:T(128)S(1)} all-reduce(f32[128]{0:T(128)S(1)} %get-tuple-element.324), channel_id=1, replica_groups=mesh['pix'=8,'frm'=4] {'pix'}, use_global_device_ids=true, to_apply=%region_11.13 | all-reduce | flops 128 | bytes 1024 | tf_op jit(solution)/shard_map/psum | solution.py:48
  318.6 17.1 %psum.187 = f32[128]{0:T(128)S(1)} all-reduce(f32[128]{0:T(128)S(1)} %get-tuple-element.326), channel_id=1, replica_groups=mesh['pix'=8,'frm'=4] {'pix'}, use_global_device_ids=true, to_apply=%region_14.16 | all-reduce | flops 128 | bytes 1024 | tf_op jit(solution)/shard_map/psum | solution.py:48
  338.1 19.2 %psum.188 = f32[128]{0:T(128)S(1)} all-reduce(f32[128]{0:T(128)S(1)} %get-tuple-element.328), channel_id=1, replica_groups=mesh['pix'=8,'frm'=4] {'pix'}, use_global_device_ids=true, to_apply=%region_17.19 | all-reduce | flops 128 | bytes 1024 | tf_op jit(solution)/shard_map/psum | solution.py:48
  359.4 17.1 %psum.189 = f32[128]{0:T(128)S(1)} all-reduce(f32[128]{0:T(128)S(1)} %get-tuple-element.330), channel_id=1, replica_groups=mesh['pix'=8,'frm'=4] {'pix'}, use_global_device_ids=true, to_apply=%region_20.22 | all-reduce | flops 128 | bytes 1024 | tf_op jit(solution)/shard_map/psum | solution.py:48
  378.9 19.3 %psum.190 = f32[128]{0:T(128)S(1)} all-reduce(f32[128]{0:T(128)S(1)} %get-tuple-element.332), channel_id=1, replica_groups=mesh['pix'=8,'frm'=4] {'pix'}, use_global_device_ids=true, to_apply=%region_23.25 | all-reduce | flops 128 | bytes 1024 | tf_op jit(solution)/shard_map/psum | solution.py:48
  400.6 17.1 %psum.191 = f32[128]{0:T(128)S(1)} all-reduce(f32[128]{0:T(128)S(1)} %get-tuple-element.334), channel_id=1, replica_groups=mesh['pix'=8,'frm'=4] {'pix'}, use_global_device_ids=true, to_apply=%region_25.27 | all-reduce | flops 128 | bytes 1024 | tf_op jit(solution)/shard_map/psum | solution.py:48
  419.4 19.1 %psum.192 = f32[128]{0:T(128)S(1)} all-reduce(f32[128]{0:T(128)S(1)} %get-tuple-element.336), channel_id=1, replica_groups=mesh['pix'=8,'frm'=4] {'pix'}, use_global_device_ids=true, to_apply=%region_27.29 | all-reduce | flops 128 | bytes 1024 | tf_op jit(solution)/shard_map/psum | solution.py:48
  440.8 17.1 %psum.193 = f32[128]{0:T(128)S(1)} all-reduce(f32[128]{0:T(128)S(1)} %get-tuple-element.338), channel_id=1, replica_groups=mesh['pix'=8,'frm'=4] {'pix'}, use_global_device_ids=true, to_apply=%region_29.31 | all-reduce | flops 128 | bytes 1024 | tf_op jit(solution)/shard_map/psum | solution.py:48
  460.2 19.1 %psum.194 = f32[128]{0:T(128)S(1)} all-reduce(f32[128]{0:T(128)S(1)} %get-tuple-element.340), channel_id=1, replica_groups=mesh['pix'=8,'frm'=4] {'pix'}, use_global_device_ids=true, to_apply=%region_31.33 | all-reduce | flops 128 | bytes 1024 | tf_op jit(solution)/shard_map/psum | solution.py:48
  481.6 17.1 %psum.195 = f32[128]{0:T(128)S(1)} all-reduce(f32[128]{0:T(128)S(1)} %get-tuple-element.342), channel_id=1, replica_groups=mesh['pix'=8,'frm'=4] {'pix'}, use_global_device_ids=true, to_apply=%region_33.35 | all-reduce | flops 128 | bytes 1024 | tf_op jit(solution)/shard_map/psum | solution.py:48
  501.0 19.1 %psum.196 = f32[128]{0:T(128)S(1)} all-reduce(f32[128]{0:T(128)S(1)} %get-tuple-element.344), channel_id=1, replica_groups=mesh['pix'=8,'frm'=4] {'pix'}, use_global_device_ids=true, to_apply=%region_35.37 | all-reduce | flops 128 | bytes 1024 | tf_op jit(solution)/shard_map/psum | solution.py:48
  522.4 17.1 %psum.197 = f32[128]{0:T(128)S(1)} all-reduce(f32[128]{0:T(128)S(1)} %get-tuple-element.346), channel_id=1, replica_groups=mesh['pix'=8,'frm'=4] {'pix'}, use_global_device_ids=true, to_apply=%region_37.39 | all-reduce | flops 128 | bytes 1024 | tf_op jit(solution)/shard_map/psum | solution.py:48
  541.9 19.1 %psum.198 = f32[128]{0:T(128)S(1)} all-reduce(f32[128]{0:T(128)S(1)} %get-tuple-element.348), channel_id=1, replica_groups=mesh['pix'=8,'frm'=4] {'pix'}, use_global_device_ids=true, to_apply=%region_39.41 | all-reduce | flops 128 | bytes 1024 | tf_op jit(solution)/shard_map/psum | solution.py:48
  563.3 17.1 %psum.199 = f32[128]{0:T(128)S(1)} all-reduce(f32[128]{0:T(128)S(1)} %get-tuple-element.350), channel_id=1, replica_groups=mesh['pix'=8,'frm'=4] {'pix'}, use_global_device_ids=true, to_apply=%region_41.43 | all-reduce | flops 128 | bytes 1024 | tf_op jit(solution)/shard_map/psum | solution.py:48
  582.1 19.1 %psum.200 = f32[128]{0:T(128)S(1)} all-reduce(f32[128]{0:T(128)S(1)} %get-tuple-element.352), channel_id=1, replica_groups=mesh['pix'=8,'frm'=4] {'pix'}, use_global_device_ids=true, to_apply=%region_43.45 | all-reduce | flops 128 | bytes 1024 | tf_op jit(solution)/shard_map/psum | solution.py:48
  603.5 17.1 %psum.201 = f32[128]{0:T(128)S(1)} all-reduce(f32[128]{0:T(128)S(1)} %get-tuple-element.354), channel_id=1, replica_groups=mesh['pix'=8,'frm'=4] {'pix'}, use_global_device_ids=true, to_apply=%region_45.47 | all-reduce | flops 128 | bytes 1024 | tf_op jit(solution)/shard_map/psum | solution.py:48
  622.9 19.1 %psum.202 = f32[128]{0:T(128)S(1)} all-reduce(f32[128]{0:T(128)S(1)} %get-tuple-element.356), channel_id=1, replica_groups=mesh['pix'=8,'frm'=4] {'pix'}, use_global_device_ids=true, to_apply=%region_47.49 | all-reduce | flops 128 | bytes 1024 | tf_op jit(solution)/shard_map/psum | solution.py:48
  644.3 17.1 %psum.203 = f32[128]{0:T(128)S(1)} all-reduce(f32[128]{0:T(128)S(1)} %get-tuple-element.358), channel_id=1, replica_groups=mesh['pix'=8,'frm'=4] {'pix'}, use_global_device_ids=true, to_apply=%region_49.51 | all-reduce | flops 128 | bytes 1024 | tf_op jit(solution)/shard_map/psum | solution.py:48
  663.8 19.1 %psum.204 = f32[128]{0:T(128)S(1)} all-reduce(f32[128]{0:T(128)S(1)} %get-tuple-element.360), channel_id=1, replica_groups=mesh['pix'=8,'frm'=4] {'pix'}, use_global_device_ids=true, to_apply=%region_51.53 | all-reduce | flops 128 | bytes 1024 | tf_op jit(solution)/shard_map/psum | solution.py:48
  704.6 19.1 %psum.206 = f32[128]{0:T(128)S(1)} all-reduce(f32[128]{0:T(128)S(1)} %get-tuple-element.364), channel_id=1, replica_groups=mesh['pix'=8,'frm'=4] {'pix'}, use_global_device_ids=true, to_apply=%region_55.57 | all-reduce | flops 128 | bytes 1024 | tf_op jit(solution)/shard_map/psum | solution.py:48
  (151 shorter events, 256.4 us)
Async XLA Ops:
  6.5 156.0 %copy-start.4 = (s32[1,256]{1,0:T(1,128)S(1)}, s32[1,256]{1,0:T(1,128)}, u32[]{:S(2)}) copy-start(s32[1,256]{1,0:T(1,128)} %param.59) | copy-start | bytes 3076
  6.5 156.2 %copy-start.3 = (s32[1024]{0:T(1024)S(1)}, s32[1024]{0:T(1024)}, u32[]{:S(2)}) copy-start(s32[1024]{0:T(1024)} %param.58) | copy-start | bytes 12292
  6.5 46.0 %all-gather.2.cloned.1.call-start = ((), (), s32[]{:S(2)}) async-start(), calls=%async_computation | async-start | bytes 1179648 | tf_op jit(solution)/shard_map/all_gather | solution.py:19
  7.3 83.4 %all-reduce.3.cloned.1.call-start = ((), (), s32[]{:S(2)}) async-start(), calls=%async_computation.1 | async-start | bytes 2097152 | tf_op jit(solution)/shard_map/psum | solution.py:23
  90.6 16.3 %collective-permute-start = (f32[128,1024]{1,0:T(8,128)}, f32[128,1024]{1,0:T(8,128)S(1)}, u32[]{:S(2)}, u32[]{:S(2)}) collective-permute-start(f32[128,1024]{1,0:T(8,128)} %get-tuple-element.294), channel_id=1, source_target_pairs={{0,4},{4,8},{8,12},{12,16},{16,20},{20,24},{24,28},{28,0},{1,5},{5... | collective-permute-start | bytes 1572872 | tf_op jit(solution)/shard_map/ppermute | solution.py:26
  106.9 15.2 %collective-permute-start.1 = (f32[128,1024]{1,0:T(8,128)S(1)}, f32[128,1024]{1,0:T(8,128)S(1)}, u32[]{:S(2)}, u32[]{:S(2)}) collective-permute-start(f32[128,1024]{1,0:T(8,128)S(1)} %collective-permute-done), channel_id=1, source_target_pairs={{0,4},{4,8},{8,12},{12,16},{16,20},{20,24},{24,28},{28,0},{1,5},{5... | collective-permute-start | bytes 1572872 | tf_op jit(solution)/shard_map/ppermute | solution.py:26
  122.1 14.3 %collective-permute-start.2 = (f32[128,1024]{1,0:T(8,128)S(1)}, f32[128,1024]{1,0:T(8,128)S(1)}, u32[]{:S(2)}, u32[]{:S(2)}) collective-permute-start(f32[128,1024]{1,0:T(8,128)S(1)} %collective-permute-done.1), channel_id=1, source_target_pairs={{0,4},{4,8},{8,12},{12,16},{16,20},{20,24},{24,28},{28,0},{1,5},{5... | collective-permute-start | bytes 1572872 | tf_op jit(solution)/shard_map/ppermute | solution.py:26
  136.4 13.5 %collective-permute-start.3 = (f32[128,1024]{1,0:T(8,128)S(1)}, f32[128,1024]{1,0:T(8,128)S(1)}, u32[]{:S(2)}, u32[]{:S(2)}) collective-permute-start(f32[128,1024]{1,0:T(8,128)S(1)} %collective-permute-done.2), channel_id=1, source_target_pairs={{0,4},{4,8},{8,12},{12,16},{16,20},{20,24},{24,28},{28,0},{1,5},{5... | collective-permute-start | bytes 1572872 | tf_op jit(solution)/shard_map/ppermute | solution.py:26
  149.9 12.6 %collective-permute-start.4 = (f32[128,1024]{1,0:T(8,128)S(1)}, f32[128,1024]{1,0:T(8,128)S(1)}, u32[]{:S(2)}, u32[]{:S(2)}) collective-permute-start(f32[128,1024]{1,0:T(8,128)S(1)} %collective-permute-done.3), channel_id=1, source_target_pairs={{0,4},{4,8},{8,12},{12,16},{16,20},{20,24},{24,28},{28,0},{1,5},{5... | collective-permute-start | bytes 1572872 | tf_op jit(solution)/shard_map/ppermute | solution.py:26
  162.5 12.3 %copy-start.1 = (f32[128,1024]{1,0:T(8,128)}, f32[128,1024]{1,0:T(8,128)S(1)}, u32[]{:S(2)}) copy-start(f32[128,1024]{1,0:T(8,128)S(1)} %collective-permute-done.4) | copy-start | bytes 1572868
  162.5 12.3 %collective-permute-start.5 = (f32[128,1024]{1,0:T(8,128)S(1)}, f32[128,1024]{1,0:T(8,128)}, u32[]{:S(2)}, u32[]{:S(2)}) collective-permute-start(f32[128,1024]{1,0:T(8,128)S(1)} %collective-permute-done.4), channel_id=1, source_target_pairs={{0,4},{4,8},{8,12},{12,16},{16,20},{20,24},{24,28},{28,0},{1,5},{5... | collective-permute-start | bytes 1572872 | tf_op jit(solution)/shard_map/ppermute | solution.py:26
  174.8 20.6 %collective-permute-start.6 = (f32[128,1024]{1,0:T(8,128)}, f32[128,1024]{1,0:T(8,128)}, u32[]{:S(2)}, u32[]{:S(2)}) collective-permute-start(f32[128,1024]{1,0:T(8,128)} %collective-permute-done.5), channel_id=1, source_target_pairs={{0,4},{4,8},{8,12},{12,16},{16,20},{20,24},{24,28},{28,0},{1,5},{5... | collective-permute-start | bytes 1572872 | tf_op jit(solution)/shard_map/ppermute | solution.py:26
  195.3 3.6 copy-start
  197.6 3.6 copy-start.2
Sparse Core Ops, SparseCore 0:
  9.5 42.9 all-gather.1
  55.5 35.0 all-reduce.2
